TPU v7x, 128 devices: a whole 4x4x4 slice. The times are simulated.
128 devices in a mesh: dp: 8 (over z_hi, y), tensor: 16 (over x, z_lo, core).
Axes of the slice: x: 4, y: 4, z: 4 (z_hi: 2, z_lo: 2; z = z_hi * 2 + z_lo), core: 2. Of those that a mesh axis runs over, the one named last changes fastest.
Arguments:
- noisy: bfloat16 [64, 256, 1152], P('dp', None, 'tensor'), may hold values from -6 to 6
- labels: int32 [64], P('dp'), may hold values from 0 to 999
- tsteps: int32 [64], P('dp'), may hold values from 0 to 999
- guide_index: int32 [64], P('dp'), may hold values from 0 to 31
- class_table: bfloat16 [1001, 1152], replicated, may hold values from -6 to 6
- time_table: bfloat16 [1000, 1152], replicated, may hold values from -6 to 6
- guide_table: bfloat16 [32, 1152], replicated, may hold values from -6 to 6
- guide_weights: float32 [32], replicated, may hold values from 0.5 to 4
- teacher_qkv: bfloat16 [1152, 3456], P(None, 'tensor'), may hold values from -0.1875 to 0.1875
- teacher_out: bfloat16 [1152, 1152], P('tensor'), may hold values from -0.1875 to 0.1875
- teacher_ada: bfloat16 [3, 1152, 1152], P(None, None, 'tensor'), may hold values from -0.1875 to 0.1875
- student_qkv: bfloat16 [1152, 3456], P(None, 'tensor'), may hold values from -0.1875 to 0.1875
- student_out: bfloat16 [1152, 1152], P('tensor'), may hold values from -0.1875 to 0.1875
- student_ada: bfloat16 [3, 1152, 1152], P(None, None, 'tensor'), may hold values from -0.1875 to 0.1875
Outputs:
- grad_qkv: float32 [1152, 3456], P('dp', 'tensor')
- grad_out: float32 [1152, 1152], P('tensor', 'dp')
- grad_ada: float32 [3, 1152, 1152], P(None, 'dp', 'tensor')
All inputs are finite; a program needn't handle non-finite values.
Results may differ from a plain program's by a relative error of at most 0.034.
Values may be sent and summed in bfloat16 or wider, within the bound.
No kernel may reach another device: no remote copies, remote signals or barrier semaphores. Data moves between devices by JAX's collectives and lax.ppermute only.
A program may use at most 128 MiB of HBM per device.

v0:
```python
import math

import jax
import jax.numpy as jnp
from jax import lax
from jax.sharding import PartitionSpec as P

HD = 72


norm_eps = 1e-06


def in_order(pieces, dim):
    shape = list(pieces.shape[1:])
    shape[dim] *= pieces.shape[0]
    return jnp.moveaxis(pieces, 0, dim).reshape(shape)


def sent_to_all(shard, axis):
    copies = jnp.broadcast_to(shard, (lax.axis_size(axis), *shard.shape))
    return lax.all_to_all(copies, axis, split_axis=0, concat_axis=0, tiled=True)


def collect(shard, axis, dim):
    return in_order(sent_to_all(shard, axis), dim)


def taken_together(shard, axis):
    return sent_to_all(shard, axis).sum(axis=0)


def in_one(arrays, axis):
    vector, at, outs = (jnp.concatenate([a.reshape(-1) for a in arrays]), 0, [])
    running = taken_together(vector, axis)
    for a in arrays:
        outs.append(running[at : at + a.size].reshape(a.shape))
        at += a.size
    return tuple(outs)


def in_blocks(shard, dim, devices):
    shape = shard.shape
    pieces = shard.reshape(*shape[:dim], devices, shape[dim] // devices, *shape[dim + 1 :])
    return jnp.moveaxis(pieces, dim, 0)


def sum_together(arrays, axis, dims):
    devices = lax.axis_size(axis)
    pieces = [in_blocks(a, dim, devices) for a, dim in zip(arrays, dims)]
    lines = jnp.concatenate([b.reshape(devices, -1) for b in pieces], axis=1)
    span = max(16, -(-lines.shape[1] // 1024) * 8)
    lines = jnp.pad(lines, ((0, 0), (0, span * 128 - lines.shape[1]))).reshape(-1, 128)
    vector, at, outs = (lax.psum_scatter(lines, axis, tiled=True).reshape(-1), 0, [])
    for b in pieces:
        part = b[0]
        outs.append(vector[at : at + part.size].reshape(part.shape))
        at += part.size
    return tuple(outs)


def lookup_rows(indices, table_rows):
    one_hot = (
        indices[:, None] == jnp.arange(table_rows.shape[0], dtype=jnp.int32)[None, :]
    ).astype(table_rows.dtype)
    return jnp.dot(one_hot, table_rows, preferred_element_type=jnp.float32)


def attend(qkv_sums, heads_here):
    batch_rows, seq_len = (qkv_sums.shape[0], qkv_sums.shape[1])
    heads_qkv = qkv_sums.astype(jnp.bfloat16).reshape(batch_rows, seq_len, heads_here, 3, HD)
    queries, key_rows, values = (
        heads_qkv[:, :, :, 0],
        heads_qkv[:, :, :, 1],
        heads_qkv[:, :, :, 2],
    )
    scores = jnp.einsum(
        "blhe,bmhe->bhlm", queries, key_rows, preferred_element_type=jnp.float32
    ) * (1.0 / math.sqrt(HD))
    exponent = jnp.exp(scores - jnp.max(scores, axis=-1, keepdims=True))
    attn_prob = exponent / jnp.sum(exponent, axis=-1, keepdims=True)
    prob_low = attn_prob.astype(jnp.bfloat16)
    attn_mixed = jnp.einsum("bhlm,bmhe->blhe", prob_low, values, preferred_element_type=jnp.float32)
    attn_mixed = attn_mixed.astype(jnp.bfloat16).reshape(batch_rows, seq_len, heads_here * HD)
    return (heads_qkv, attn_prob, prob_low, attn_mixed)


def attend_grad(heads_qkv, attn_prob, prob_low, grad_low):
    batch_rows, seq_len = (heads_qkv.shape[0], heads_qkv.shape[1])
    queries, key_rows, values = (
        heads_qkv[:, :, :, 0],
        heads_qkv[:, :, :, 1],
        heads_qkv[:, :, :, 2],
    )
    grad_probs = jnp.einsum("blhe,bmhe->bhlm", grad_low, values, preferred_element_type=jnp.float32)
    row_delta = jnp.sum(attn_prob * grad_probs, axis=-1, keepdims=True)
    grad_scores = (attn_prob * (grad_probs - row_delta) * (1.0 / math.sqrt(HD))).astype(
        jnp.bfloat16
    )
    grad_query = jnp.einsum(
        "bhlm,bmhe->blhe", grad_scores, key_rows, preferred_element_type=jnp.float32
    )
    grad_keys = jnp.einsum(
        "bhlm,blhe->bmhe", grad_scores, queries, preferred_element_type=jnp.float32
    )
    grad_values = jnp.einsum(
        "bhlm,blhe->bmhe", prob_low, grad_low, preferred_element_type=jnp.float32
    )
    grad_qkv_act = jnp.stack([grad_query, grad_keys, grad_values], axis=3).astype(jnp.bfloat16)
    return grad_qkv_act.reshape(batch_rows, seq_len, -1)


def forward(source, embed_act, qkv_weight, out_weight, ada_weight):
    heads_here = out_weight.shape[0] // HD
    modulation = jnp.einsum(
        "bd,kde->bke", embed_act, ada_weight, preferred_element_type=jnp.float32
    )
    wide_mod = collect(modulation, "tensor", 2)
    full_rows = (
        source.astype(jnp.float32) * (1.0 + wide_mod[:, 1][:, None]) + wide_mod[:, 0][:, None]
    ).astype(jnp.bfloat16)
    qkv_sums = jnp.einsum("bld,df->blf", full_rows, qkv_weight, preferred_element_type=jnp.float32)
    heads_qkv, attn_prob, prob_low, attn_mixed = attend(qkv_sums, heads_here)
    partial_value = jnp.einsum(
        "blf,fd->bld", attn_mixed, out_weight, preferred_element_type=jnp.float32
    )
    projected = lax.psum_scatter(
        partial_value.astype(jnp.bfloat16), "tensor", scatter_dimension=2, tiled=True
    ).astype(jnp.float32)
    branch = modulation[:, 2][:, None] * projected
    return (branch, (full_rows, heads_qkv, attn_prob, prob_low, attn_mixed, projected, modulation))


def local(
    noisy,
    labels,
    tsteps,
    guide_index,
    class_table,
    time_table,
    guide_table,
    guide_weights,
    teacher_qkv,
    teacher_out,
    teacher_ada,
    student_qkv,
    student_out,
    student_ada,
):
    samples, seq_len, width_part = noisy.shape
    model_width = width_part * lax.axis_size("tensor")
    batch_size = samples * lax.axis_size("dp")
    signal = noisy.astype(jnp.float32)
    row_sums = in_one((jnp.sum(signal, axis=2), jnp.sum(signal * signal, axis=2)), "tensor")
    row_mean = row_sums[0] / model_width
    row_var = row_sums[1] / model_width - row_mean * row_mean
    normed = ((signal - row_mean[:, :, None]) * lax.rsqrt(row_var + norm_eps)[:, :, None]).astype(
        jnp.bfloat16
    )
    null_class = class_table.shape[0] - 1
    time_embed = lookup_rows(tsteps, time_table)
    cond_embed = lookup_rows(labels, class_table) + time_embed
    null_embed = class_table[null_class].astype(jnp.float32)[None, :] + time_embed
    guide_hot = guide_index[:, None] == jnp.arange(guide_table.shape[0], dtype=jnp.int32)[None, :]
    student_embed = cond_embed + jnp.dot(
        guide_hot.astype(jnp.bfloat16), guide_table, preferred_element_type=jnp.float32
    )
    strength = jnp.sum(jnp.where(guide_hot, guide_weights[None, :], 0.0), axis=1)
    cond_act = jax.nn.silu(cond_embed).astype(jnp.bfloat16)
    null_act = jax.nn.silu(null_embed).astype(jnp.bfloat16)
    student_act = jax.nn.silu(student_embed).astype(jnp.bfloat16)
    scale_norm = 1.0 / math.sqrt(batch_size * seq_len)
    wide_rows = lax.all_gather(normed, "tensor", axis=2, tiled=True)
    teacher_full = jnp.concatenate([wide_rows, wide_rows], axis=0)
    teacher_act = jnp.concatenate([cond_act, null_act], axis=0)
    teacher_branch, unused_saved = forward(
        teacher_full, teacher_act, teacher_qkv, teacher_out, teacher_ada
    )
    teacher_update = teacher_branch.astype(jnp.bfloat16).astype(jnp.float32)
    scaled = strength[:, None, None]
    target = signal + (
        (1.0 + scaled) * teacher_update[:samples] - scaled * teacher_update[samples:]
    )
    branch, saved = forward(wide_rows, student_act, student_qkv, student_out, student_ada)
    full_rows, heads_qkv, attn_prob, prob_low, attn_mixed, projected, modulation = saved
    heads_here = student_out.shape[0] // HD
    cotangent = (signal + branch - target) * scale_norm
    grad_gate = jnp.sum(cotangent * projected, axis=1)
    grad_proj = (cotangent * modulation[:, 2][:, None]).astype(jnp.bfloat16)
    gathered = lax.all_gather(grad_proj, "tensor", axis=2, tiled=True)
    grad_mixed = jnp.einsum(
        "bld,ed->ble", gathered, student_out, preferred_element_type=jnp.float32
    )
    block_grad = jnp.einsum("ble,bld->ed", attn_mixed, gathered, preferred_element_type=jnp.float32)
    grad_mixed, grad_out_rows = (grad_mixed, block_grad)
    grad_low = grad_mixed.astype(jnp.bfloat16).reshape(samples, seq_len, heads_here, HD)
    grad_qkv_act = attend_grad(heads_qkv, attn_prob, prob_low, grad_low)
    grad_qkv_local = jnp.einsum(
        "bld,blf->df", full_rows, grad_qkv_act, preferred_element_type=jnp.float32
    )
    input_terms = jnp.einsum(
        "blf,df->bld", grad_qkv_act, student_qkv, preferred_element_type=jnp.float32
    )
    grad_input = lax.psum_scatter(
        input_terms.astype(jnp.bfloat16), "tensor", scatter_dimension=2, tiled=True
    ).astype(jnp.float32)
    grad_shift = jnp.sum(grad_input, axis=1)
    grad_scale = jnp.sum(grad_input * normed.astype(jnp.float32), axis=1)
    grad_modulation = jnp.stack([grad_shift, grad_scale, grad_gate], axis=1)
    grad_ada_local = jnp.einsum("bd,bke->kde", student_act.astype(jnp.float32), grad_modulation)
    grad_qkv, grad_out, grad_ada = tuple(
        (
            part.astype(jnp.float32)
            for part in sum_together(
                (
                    grad_qkv_local.astype(jnp.bfloat16),
                    grad_out_rows.astype(jnp.bfloat16),
                    grad_ada_local.astype(jnp.bfloat16),
                ),
                "dp",
                (0, 1, 1),
            )
        )
    )
    return (grad_qkv, grad_out, grad_ada)


def solution(mesh):
    return jax.shard_map(
        local,
        mesh=mesh,
        in_specs=(
            P("dp", None, "tensor"),
            P("dp"),
            P("dp"),
            P("dp"),
            P(),
            P(),
            P(),
            P(),
            P(None, "tensor"),
            P("tensor", None),
            P(None, None, "tensor"),
            P(None, "tensor"),
            P("tensor", None),
            P(None, None, "tensor"),
        ),
        out_specs=(P("dp", "tensor"), P("tensor", "dp"), P(None, "dp", "tensor")),
        check_vma=False,
    )
```

profile of v0, /device:TPU:0, one launch (start us, length us, event | category | flops | bytes accessed | tf_op | source)
XLA Modules:
  0.0 496.4 jit_solution(3670786287526547354)
XLA Ops:
  8.7 13.3 %all_to_all.16 = f32[16,1,4096]{2,1,0:T(1,128)S(1)} all-to-all(f32[16,1,4096]{2,1,0:T(1,128)S(1)} %broadcast_in_dim.14), channel_id=1, replica_groups=mesh['dp'=8,'tensor'=16] {'tensor'}, dimensions={0} | all-to-all | bytes 524288 | tf_op jit(solution)/shard_map/all_to_all | solution.py:22
  26.8 9.7 %all_to_all.17 = f32[16,8,3,72]{3,1,2,0:T(8,128)S(1)} all-to-all(f32[16,8,3,72]{3,1,2,0:T(8,128)S(1)} %broadcast_in_dim.19), channel_id=1, replica_groups=mesh['dp'=8,'tensor'=16] {'tensor'}, dimensions={0} | all-to-all | bytes 221184 | tf_op jit(solution)/shard_map/all_to_all | solution.py:22
  36.7 25.5 %all-gather.3.cloned.1.call-done = bf16[8,256,1152]{1,2,0:T(8,128)(2,1)} async-done(((bf16[8,256,72]{1,2,0:T(8,128)(2,1)}), bf16[8,256,1152]{1,2,0:T(8,128)(2,1)}) %all-gather.3.cloned.1.call-update) | async-done | bytes 4718608 | tf_op jit(solution)/shard_map/all_gather | solution.py:173
  62.2 5.5 %fusion.34 = bf16[8,256,216]{1,2,0:T(8,128)(2,1)S(1)} fusion(bf16[8,256,1152]{1,2,0:T(8,128)(2,1)} %all-gather.3.cloned.1.call-done, f32[8,1152]{1,0:T(8,128)S(1)} %get-tuple-element.14, f32[8,1152]{1,0:T(8,128)S(1)} %get-tuple-element.13, bf16[1152,216]{0,1:T(8,128)(2,1)S(1)} %copy-done.5), kind=kOutput, calls=%fused_computation.43 | convolution fusion | flops 1029095424 | bytes 6174720 | tf_op jit(solution)/shard_map/bld,df->blf/dot_general | solution.py:122
  67.7 2.3 fusion.101
  70.0 2.0 fusion.49
  73.4 2.9 copy.153
  77.6 13.5 %all_to_all.18 = f32[16,16,3,72]{3,1,2,0:T(8,128)S(1)} all-to-all(f32[16,16,3,72]{3,1,2,0:T(8,128)S(1)} %broadcast_in_dim.22), channel_id=1, replica_groups=mesh['dp'=8,'tensor'=16] {'tensor'}, dimensions={0} | all-to-all | bytes 442368 | tf_op jit(solution)/shard_map/all_to_all | solution.py:22
  91.5 9.6 %fusion.27 = bf16[16,256,216]{1,2,0:T(8,128)(2,1)S(1)} fusion(bf16[8,256,1152]{1,2,0:T(8,128)(2,1)} %all-gather.3.cloned.1.call-done, f32[16,1152]{1,0:T(8,128)S(1)} %get-tuple-element.12, f32[16,1152]{1,0:T(8,128)S(1)} %get-tuple-element.11, bf16[1152,216]{0,1:T(8,128)(2,1)} %param.22), kind=kOutput, calls=%fused_computation.40 | convolution fusion | flops 2062909440 | bytes 7133184 | tf_op jit(solution)/shard_map/bld,df->blf/dot_general | solution.py:122
  101.9 3.0 fusion.100
  104.9 8.1 %fusion.102 = bf16[144,8,16,256]{3,1,0,2:T(8,128)(2,1)} fusion(bf16[72,1152]{1,0:T(8,128)(2,1)S(1)} %copy-done.11, f32[16,256,256]{1,2,0:T(8,128)} %get-tuple-element.22, f32[16,256]{1,0:T(8,128)S(1)} %get-tuple-element.21, bf16[16,256,1,3,72]{1,4,3,0,2:T(8,128)(2,1)S(1)} %bitcast.225), kind=kOutput, calls=%fused_computation.151 | convolution fusion | flops 837582848 | bytes 14403584 | tf_op jit(solution)/shard_map/blf,fd->bld/dot_general | solution.py:124
  113.0 8.7 %copy.155 = bf16[144,8,16,256]{3,1,2,0:T(8,128)(2,1)} copy(bf16[144,8,16,256]{3,1,0,2:T(8,128)(2,1)} %fusion.102) | data formatting | bytes 18874368
  122.6 24.5 %reduce-scatter.10.cloned.1.call-done = bf16[72,2048]{1,0:T(8,128)(2,1)} async-done(((bf16[1152,2048]{1,0:T(8,128)(2,1)}), bf16[72,2048]{1,0:T(8,128)(2,1)}) %reduce-scatter.10.cloned.1.call-update) | async-done | bytes 294928
  148.1 106.4 %reduce-scatter.12.cloned.1.call-done = bf16[72,4096]{1,0:T(8,128)(2,1)} async-done(((bf16[1152,4096]{1,0:T(8,128)(2,1)}), bf16[72,4096]{1,0:T(8,128)(2,1)}) %reduce-scatter.12.cloned.1.call-update) | async-done | bytes 589840
  257.1 42.0 %all-gather.5.cloned.1.call-done = bf16[8,256,1152]{1,2,0:T(8,128)(2,1)} async-done(((bf16[8,256,72]{1,2,0:T(8,128)(2,1)}), bf16[8,256,1152]{1,2,0:T(8,128)(2,1)}) %all-gather.5.cloned.1.call-update) | async-done | bytes 4718608 | tf_op jit(solution)/shard_map/all_gather | solution.py:190
  299.2 3.4 convolution_convert_fusion.4
  303.1 2.8 fusion.71
  305.9 4.5 fusion.43
  310.4 4.4 fusion.46
  316.4 2.8 copy.157
  319.6 3.9 fusion.20
  324.8 5.2 %fusion.15 = bf16[1152,216]{0,1:T(8,128)(2,1)S(1)} fusion(bf16[8,256,216]{1,2,0:T(8,128)(2,1)S(1)} %bitcast.215, bf16[8,256,1152]{1,2,0:T(8,128)(2,1)} %all-gather.3.cloned.1.call-done, f32[8,1152]{1,0:T(8,128)S(1)} %get-tuple-element.14, f32[8,1152]{1,0:T(8,128)S(1)} %get-tuple-element.13), kind=kOutput, calls=%fused_computation.22 | convolution fusion | flops 1028901888 | bytes 6174720 | tf_op jit(solution)/shard_map/bld,blf->df/dot_general | solution.py:198
  332.0 57.0 %reduce-scatter.14.cloned.1.call-done = bf16[72,2048]{1,0:T(8,128)(2,1)} async-done(((bf16[1152,2048]{1,0:T(8,128)(2,1)}), bf16[72,2048]{1,0:T(8,128)(2,1)}) %reduce-scatter.14.cloned.1.call-update) | async-done | bytes 294928
  399.6 85.9 %all-reduce.4.cloned.1.call-done = bf16[4544,128]{1,0:T(8,128)(2,1)} async-done(((bf16[4544,128]{1,0:T(8,128)(2,1)}), bf16[4544,128]{1,0:T(8,128)(2,1)}) %all-reduce.4.cloned.1.call-update) | async-done | bytes 1163280
  (106 shorter events, 34.2 us)
Async XLA Ops:
  7.2 17.8 %copy-start = (bf16[1000,1152]{1,0:T(8,128)(2,1)S(1)}, bf16[1000,1152]{1,0:T(8,128)(2,1)}, u32[]{:S(2)}) copy-start(bf16[1000,1152]{1,0:T(8,128)(2,1)} %param.19) | copy-start | bytes 6912004
  7.2 17.8 %copy-start.10 = (s32[8]{0:T(128)S(1)}, s32[8]{0:T(128)}, u32[]{:S(2)}) copy-start(s32[8]{0:T(128)} %param.16) | copy-start | bytes 100
  7.2 55.0 %all-gather.3.cloned.1.call-start = ((), (), s32[]{:S(2)}) async-start(), calls=%async_computation.6 | async-start | bytes 5013504 | tf_op jit(solution)/shard_map/all_gather | solution.py:173
  8.5 17.1 %copy-start.9 = (s32[8]{0:T(128)S(1)}, s32[8]{0:T(128)}, u32[]{:S(2)}) copy-start(s32[8]{0:T(128)} %param.15) | copy-start | bytes 100
  24.0 123.1 %reduce-scatter.10.cloned.1.call-start = ((), (), s32[]{:S(2)}) async-start(), calls=%async_computation.8 | async-start | bytes 5013504
  24.1 1.7 copy-start.3
  25.0 1.2 copy-start.12
  25.0 1.2 copy-start.13
  25.0 1.4 copy-start.6
  25.8 36.4 %copy-start.5 = (bf16[1152,216]{0,1:T(8,128)(2,1)S(1)}, bf16[1152,216]{0,1:T(8,128)(2,1)}, u32[]{:S(2)}) copy-start(bf16[1152,216]{0,1:T(8,128)(2,1)} %param.25) | copy-start | bytes 1492996
  67.7 4.2 copy-start.8
  69.9 2.0 copy-start.4
  76.3 1.0 copy-start.7
  76.3 178.2 %reduce-scatter.12.cloned.1.call-start = ((), (), s32[]{:S(2)}) async-start(), calls=%async_computation.9 | async-start | bytes 10027008
  101.9 3.0 copy-start.11
  121.7 0.7 copy-start.14
  121.7 134.2 %copy-start.2 = (bf16[8,256,72]{1,2,0:T(8,128)(2,1)S(1)}, bf16[8,256,72]{1,2,0:T(8,128)(2,1)}, u32[]{:S(2)}) copy-start(bf16[8,256,72]{1,2,0:T(8,128)(2,1)} %param.14) | copy-start | bytes 884740
  121.7 177.4 %all-gather.5.cloned.1.call-start = ((), (), s32[]{:S(2)}) async-start(), calls=%async_computation.7 | async-start | bytes 5013504 | tf_op jit(solution)/shard_map/all_gather | solution.py:190
  257.1 132.0 %reduce-scatter.14.cloned.1.call-start = ((), (), s32[]{:S(2)}) async-start(), calls=%async_computation.10 | async-start | bytes 5013504
  299.2 3.4 copy-start.16
  319.3 166.2 %all-reduce.4.cloned.1.call-start = ((), (), s32[]{:S(2)}) async-start(), calls=%async_computation.11 | async-start | bytes 2326528
  395.2 94.4 %copy-start.1 = (bf16[1000,1152]{1,0:T(8,128)(2,1)S(1)}, bf16[1000,1152]{1,0:T(8,128)(2,1)}, u32[]{:S(2)}) copy-start(bf16[1000,1152]{1,0:T(8,128)(2,1)} %param.19) | copy-start | bytes 6912004
  396.7 1.6 copy-start.15
Sparse Core Ops, SparseCore 0:
  24.2 37.9 all-gather.2
  76.4 70.6 reduce-scatter.9
  149.5 104.9 reduce-scatter.11
  257.2 41.9 all-gather.4
  319.4 69.5 reduce-scatter.13
  398.4 86.9 all-reduce.3
where the time goes:
time: 497 us; the launch traced here: 496 us
  waiting for transfers between devices  341 us (69%)
  matrix products  57.8 us (12%)
  blocking collectives  36.5 us (7%)
  local copies, waits for them, and re-layouts  32.6 us (7%)
  between operations  15.2 us (3%)
  other arithmetic  12.4 us (2%)
    unnamed x10, waiting for transfers between devices  274 us
    all_gather x1, waiting for transfers between devices, local(): gathered = lax.all_gather(grad_proj, 'tensor', axis=2, tiled=True)  42 us
    all_to_all x3, blocking collectives, sent_to_all(): return lax.all_to_all(copies, axis, split_axis=0, concat_axis=0, tiled=True)  36.5 us
    all_gather x1, waiting for transfers between devices, local(): wide_rows = lax.all_gather(normed, 'tensor', axis=2, tiled=True)  25.5 us
    unnamed x43, local copies, waits for them, and re-layouts  19.9 us
    dot_general x2, matrix products, forward(): jnp.einsum('bld,df->blf', full_rows, qkv_weight, preferred_element_type=j...  15.1 us
  transfers between devices with their start and end apart: 6, of which 6 were waited for; matrix products, arithmetic and copies ran while one was open for 10% of the time, Pallas kernels for 0%

commit v1 on v0

v1 whole, which is shorter than its diff:
```python
import functools
import math

import jax
import jax.numpy as jnp
from jax import lax
from jax.experimental import pallas as pl
from jax.experimental.pallas import tpu as pltpu
from jax.sharding import Mesh
from jax.sharding import PartitionSpec as P

HD = 72
EPS = 1e-06
HEADS_HERE = 4
QKV = 3 * HD
F32 = jnp.float32
BF16 = jnp.bfloat16
SIZES = (2, 4, 4, 2, 2)
AXES = ("zhi", "y", "x", "zlo", "core")
DP = ("zhi", "y")
TENSOR = ("x", "zlo", "core")
QUAD = ("zlo", "core")
LANES = 384
KEPT = 40
INV_SQRT = 1.0 / math.sqrt(HD)


VM = pl.BlockSpec(memory_space=pltpu.VMEM)
SM = pl.BlockSpec(memory_space=pltpu.SMEM)


def params(mib, **kw):
    return pltpu.CompilerParams(vmem_limit_bytes=mib * 1024 * 1024, **kw)


def cost(us):
    return pl.CostEstimate(flops=int(us * 1e8), bytes_accessed=1000000, transcendentals=0)


def dot(a, b, ca, cb):
    return lax.dot_general(a, b, (((ca,), (cb,)), ((), ())), preferred_element_type=F32)


def shifted(n, k):
    return [(i, (i + k) % n) for i in range(n)]


def xored(n, k):
    return [(i, i ^ k) for i in range(n)]


def place(pos, pieces, whole):
    for shift, piece in zip((0, 3, 1, 2), pieces):
        rows = piece.shape[0]
        at = lax.rem(pos + shift, 4) * rows
        whole[pl.ds(pl.multiple_of(at, 32), rows), :] = piece[...]


def assemble_kernel(*refs):
    sources, (wq, wo), sems = refs[:8], refs[8:10], refs[10]
    copies = []
    for r in range(4):
        copies.append((sources[2 * r], wq.at[pl.ds(r * QKV, QKV), :]))
        copies.append((sources[2 * r + 1], wo.at[pl.ds(r * HD, HD), :]))
    copies = [pltpu.make_async_copy(a, b, sems.at[i]) for i, (a, b) in enumerate(copies)]
    for c in copies:
        c.start()
    for c in copies:
        c.wait()


def heads_forward(qkv_ref, mixed_ref, prob_ref):
    for h in range(HEADS_HERE):
        base = h * QKV
        q = qkv_ref[base : base + HD, :]
        k = qkv_ref[base + HD : base + 2 * HD, :]
        v = qkv_ref[base + 2 * HD : base + 3 * HD, :]
        s = dot(k, q, 0, 0) * INV_SQRT
        e = jnp.exp(s - jnp.max(s, axis=0, keepdims=True))
        prob = (e * (1.0 / jnp.sum(e, axis=0, keepdims=True))).astype(BF16)
        if prob_ref is not None:
            prob_ref[h] = prob
        mixed_ref[h * HD : (h + 1) * HD, :] = dot(v, prob, 1, 0).astype(BF16)


def student_kernel(
    image, col, scale_norm, pos_ref, p0, p1, p2, p3, mod_ref, wq_ref, wo_ref,
    normed_ref, modulated_ref, qkv_ref, prob_ref, mixed_ref, proj_ref, c_ref, x_ref,
):
    place(pos_ref[0], [p.at[image] for p in (p0, p1, p2, p3)], x_ref)
    width = x_ref.shape[0]
    x = x_ref[...].astype(F32)
    mean = jnp.sum(x, axis=0, keepdims=True) / width
    var = jnp.sum(x * x, axis=0, keepdims=True) / width - mean * mean
    normed = ((x - mean) * lax.rsqrt(var + EPS)).astype(BF16)
    normed_ref[...] = normed
    shift = mod_ref[:, col : col + 1]
    scale = mod_ref[:, col + 1 : col + 2]
    modulated_ref[...] = (normed.astype(F32) * (1.0 + scale) + shift).astype(BF16)
    qkv_ref[...] = dot(wq_ref[...], modulated_ref[...], 1, 0).astype(BF16)
    heads_forward(qkv_ref, mixed_ref, prob_ref)
    proj = dot(wo_ref[...], mixed_ref[...], 0, 0)
    proj_ref[...] = proj.astype(BF16)
    c_ref[...] = proj * (mod_ref[:, col + 2 : col + 3] * scale_norm)


def teacher_kernel(
    cols, pos_ref, coef_ref, normed_ref, mod_ref, wq_ref, wo_ref, cs_ref,
    o0, o1, o2, o3, acc_ref, modulated_ref, qkv_ref, mixed_ref,
):
    kind = pl.program_id(0)

    @pl.when(kind == 0)
    def _():
        acc_ref[...] = cs_ref[...]

    def column(m):
        return jnp.where(
            kind == 0, mod_ref[:, cols[0] + m : cols[0] + m + 1], mod_ref[:, cols[1] + m : cols[1] + m + 1]
        )

    modulated_ref[...] = (normed_ref[...].astype(F32) * (1.0 + column(1)) + column(0)).astype(BF16)
    qkv_ref[...] = dot(wq_ref[...], modulated_ref[...], 1, 0).astype(BF16)
    heads_forward(qkv_ref, mixed_ref, None)
    acc_ref[...] += dot(wo_ref[...], mixed_ref[...], 0, 0) * (column(2) * coef_ref[kind])

    @pl.when(kind == 1)
    def _():
        rows = o0.shape[0]
        for shift, out in zip((0, 1, 3, 2), (o0, o1, o2, o3)):
            at = lax.rem(pos_ref[0] + shift, 4) * rows
            out[...] = acc_ref[pl.ds(pl.multiple_of(at, 32), rows), :].astype(BF16)


def backward_kernel(
    col, pos_ref, p0, p1, p2, p3, mod_ref, wq_ref, wo_ref, normed_ref, qkv_ref, prob_ref, mixed_ref, proj_ref,
    gp_ref, gqkv_ref, rows_ref, cot_ref, glow_ref, gm_ref,
):
    place(pos_ref[0], (p0, p1, p2, p3), cot_ref)
    cot = cot_ref[...].astype(F32)
    gm_ref[:, 2:3] = jnp.sum(cot * proj_ref[...].astype(F32), axis=1, keepdims=True)
    gp_ref[...] = (cot * mod_ref[:, col + 2 : col + 3]).astype(BF16)
    glow_ref[...] = dot(wo_ref[...], gp_ref[...], 1, 0).astype(BF16)
    for h in range(HEADS_HERE):
        base = h * QKV
        q = qkv_ref[base : base + HD, :]
        k = qkv_ref[base + HD : base + 2 * HD, :]
        v = qkv_ref[base + 2 * HD : base + 3 * HD, :]
        g = glow_ref[h * HD : (h + 1) * HD, :]
        low = prob_ref[h]
        prob = low.astype(F32)
        gprob = dot(v, g, 0, 0)
        delta = jnp.sum(prob * gprob, axis=0, keepdims=True)
        gs = (prob * (gprob - delta) * INV_SQRT).astype(BF16)
        gqkv_ref[base : base + HD, :] = dot(k, gs, 1, 0).astype(BF16)
        gqkv_ref[base + HD : base + 2 * HD, :] = dot(q, gs, 1, 1).astype(BF16)
        gqkv_ref[base + 2 * HD : base + 3 * HD, :] = dot(g, low, 1, 1).astype(BF16)
    gin = dot(wq_ref[...], gqkv_ref[...], 0, 0)
    gm_ref[:, 0:1] = jnp.sum(gin, axis=1, keepdims=True)
    gm_ref[:, 1:2] = jnp.sum(gin * normed_ref[...].astype(F32), axis=1, keepdims=True)
    gm_ref[:, 3:] = jnp.zeros((gm_ref.shape[0], 125), F32)
    rows_ref[...] = gm_ref[...].T[:8]


def weight_grad(slot, operands, hq, ho):
    (m0, g0, p0, x0), (m1, g1, p1, x1) = operands
    a, b = slot * QKV, (slot + 1) * QKV
    hq[:, 0:QKV] = (dot(m0[...], g0[a:b, :], 1, 1) + dot(m1[...], g1[a:b, :], 1, 1)).astype(hq.dtype)
    a, b = slot * HD, (slot + 1) * HD
    ho[:, 0:HD] = (dot(p0[...], x0[a:b, :], 1, 1) + dot(p1[...], x1[a:b, :], 1, 1)).astype(ho.dtype)


def grads_kernel(m0, g0, p0, x0, m1, g1, p1, x1, s1, s3, s0, s2):
    for slot, out in ((1, s1), (3, s3), (0, s0), (2, s2)):
        weight_grad(slot, ((m0, g0, p0, x0), (m1, g1, p1, x1)), out.at[:, 0:256], out.at[:, 256:384])


def fold_kernel(at_ref, s0, s2, r1, r3, act_ref, a0, a1, a2, a3, out_ref):
    rows = (out_ref.shape[1] - 16) * 6 // 7
    width = a0.shape[1]
    summed = a0[...] + a1[...] + a2[...] + a3[...]
    side = lax.broadcasted_iota(jnp.int32, (16, 128), 1)
    part = rows // 6
    lane = lax.broadcasted_iota(jnp.int32, (rows, 128), 1)
    few = lane[:part]
    for dz, own, received in ((0, s0, r1), (1, s2, r3)):
        zlo = at_ref[1] if dz == 0 else 1 - at_ref[1]
        start = (at_ref[0] * 4 + zlo * 2 + at_ref[2]) * HD
        mine = pltpu.roll(summed, lax.rem(width - start, width), 1)[:, 0:128]
        mine = pltpu.roll(mine, 16, 1)

        def block(i, carry, own=own, received=received, zlo=zlo, mine=mine):
            at = pl.ds(pl.multiple_of(i * rows, 16), rows)
            q0 = own[at, 0:128].astype(F32) + received[at, 0:128].astype(F32)
            q1 = own[at, 128:256].astype(F32) + received[at, 128:256].astype(F32)
            o = own[at, 256:384].astype(F32) + received[at, 256:384].astype(F32)
            q1 = jnp.where(lane < QKV - 128, q1, pltpu.roll(o, QKV - 128, 1))
            low = jnp.zeros((part, 128), F32)
            high = jnp.zeros((part, 128), F32)
            for g in range(6):
                piece = pltpu.roll(o[g * part : (g + 1) * part], (32 * g - KEPT) % 128, 1)
                here = (few >= 32 * (g % 4)) & (few < 32 * (g % 4) + 32)
                if g < 4:
                    low = jnp.where(here, piece, low)
                else:
                    high = jnp.where(here, piece, high)
            dest = 2 * i + zlo
            out_ref[dest, 0:rows, 0:128] = q0.astype(BF16)
            out_ref[dest, 0:rows, 128:256] = q1.astype(BF16)
            out_ref[dest, rows : rows + part, 0:128] = low.astype(BF16)
            out_ref[dest, rows : rows + part, 128:256] = high.astype(BF16)
            right = act_ref[i, :, 128:256].astype(F32)
            right = jnp.where((side >= 16) & (side < 16 + HD), mine, right)
            out_ref[dest, rows + part :, 0:128] = act_ref[i, :, 0:128]
            out_ref[dest, rows + part :, 128:256] = right.astype(BF16)
            return carry

        lax.fori_loop(0, 8, block, 0)


def final_kernel(in_ref, gq, go, ga, side_ref):
    rows = gq.shape[0]
    part = rows // 6
    lane = lax.broadcasted_iota(jnp.int32, (part, 128), 1)

    def total(a, b, c):
        out = in_ref[0, a:b, c : c + 128].astype(F32)
        for i in range(1, in_ref.shape[0]):
            out = out + in_ref[i, a:b, c : c + 128].astype(F32)
        return out

    gq[:, 0:128] = total(0, rows, 0)
    right = total(0, rows, 128)
    gq[:, 128:QKV] = right[:, 0 : QKV - 128]
    rest = (total(rows, rows + part, 0), total(rows, rows + part, 128))
    first = pltpu.roll(right, 128 - (QKV - 128), 1)
    for g in range(6):
        tail = pltpu.roll(rest[g // 4], (KEPT - 32 * g) % 128, 1)
        both = jnp.where(lane < KEPT, first[g * part : (g + 1) * part], tail)
        go[g * part : (g + 1) * part, :] = both[:, 0:HD]
    for i in range(in_ref.shape[0]):
        side_ref[i * 16 : (i + 1) * 16, :] = in_ref[i, rows + part :, :]
    right = side_ref[:, 128:256]
    kind = lax.rem(lax.broadcasted_iota(jnp.int32, right.shape, 0), 8)
    for k in range(3):
        chosen = jnp.where(kind // 2 == k, right.astype(F32), 0.0).astype(BF16)
        grad = pltpu.roll(dot(side_ref[...], chosen, 0, 0)[:rows], 128 - 16, 1)
        ga[k] = grad[:, 0:HD]


def lookup_rows(indices, table_rows):
    one_hot = (
        indices[:, None] == jnp.arange(table_rows.shape[0], dtype=jnp.int32)[None, :]
    ).astype(table_rows.dtype)
    return jnp.dot(one_hot, table_rows, preferred_element_type=F32)


def unshuffled(pieces, zlo, core):
    outs = []
    for p in range(4):
        near = jnp.where(core == 0, pieces[p], pieces[p ^ 1])
        far = jnp.where(core == 0, pieces[p ^ 2], pieces[p ^ 3])
        outs.append(jnp.where(zlo == 0, near, far))
    return outs


def around(v):
    return tuple(lax.ppermute(v, "x", shifted(4, k)) for k in (1, 3, 2))


def all_heads(qkv_rows, out_rows, way):
    own = (qkv_rows, out_rows)
    near = tuple(lax.ppermute(v, "core", xored(2, 1)) for v in own)
    far = tuple(lax.ppermute(v, ("zhi", "zlo"), shifted(4, way)) for v in own)
    last = tuple(lax.ppermute(v, "core", xored(2, 1)) for v in far)
    width = qkv_rows.shape[1]
    return pl.pallas_call(
        assemble_kernel,
        out_shape=(
            jax.ShapeDtypeStruct((4 * QKV, width), BF16),
            jax.ShapeDtypeStruct((4 * HD, width), BF16),
        ),
        in_specs=[pl.BlockSpec(memory_space=pl.ANY)] * 8,
        out_specs=(VM, VM),
        scratch_shapes=[pltpu.SemaphoreType.DMA((8,))],
        compiler_params=params(8),
        cost_estimate=cost(2),
    )(*own, *near, *far, *last)


def local(
    noisy, labels, tsteps, guide_index, class_table, time_table, guide_table, guide_weights,
    teacher_qkv, teacher_out, teacher_ada, student_qkv, student_out, student_ada,
):
    samples, seq_len, part = noisy.shape
    width = part * 16
    block = width // 4
    x_at = lax.axis_index("x")
    zlo, core = lax.axis_index("zlo"), lax.axis_index("core")
    quad = zlo * 2 + core
    scale_norm = 1.0 / math.sqrt(samples * 8 * seq_len)
    pos = x_at.reshape(1).astype(jnp.int32)

    flipped = jnp.swapaxes(noisy, 1, 2)
    sent = [lax.dynamic_slice_in_dim(flipped, (quad ^ r) * 2, 2, 0) for r in range(4)]
    got = [sent[0]] + [lax.ppermute(sent[r], QUAD, xored(4, r)) for r in (3, 2, 1)][::-1]
    mine = jnp.concatenate(unshuffled(got, zlo, core), axis=1)
    tokens = (mine,) + around(mine)

    weights = (jnp.swapaxes(student_qkv, 0, 1), student_out, jnp.swapaxes(teacher_qkv, 0, 1), teacher_out)
    weights = lax.optimization_barrier((weights, sent))[0]
    wq_s, wo_s = all_heads(weights[0], weights[1], 3)
    wq_t, wo_t = all_heads(weights[2], weights[3], 1)

    null_class = class_table.shape[0] - 1
    time_embed = lookup_rows(tsteps, time_table)
    cond_embed = lookup_rows(labels, class_table) + time_embed
    null_embed = class_table[null_class].astype(F32)[None, :] + time_embed
    guide_hot = guide_index[:, None] == jnp.arange(guide_table.shape[0], dtype=jnp.int32)[None, :]
    student_embed = cond_embed + jnp.dot(
        guide_hot.astype(BF16), guide_table, preferred_element_type=F32
    )
    strength = jnp.sum(jnp.where(guide_hot, guide_weights[None, :], 0.0), axis=1)
    cond_act = jax.nn.silu(cond_embed).astype(BF16)
    null_act = jax.nn.silu(null_embed).astype(BF16)
    student_act = jax.nn.silu(student_embed).astype(BF16)
    mod_t = jnp.einsum(
        "bd,kde->bke", jnp.concatenate([cond_act, null_act], axis=0), teacher_ada, preferred_element_type=F32
    )
    mod_s = jnp.einsum("bd,kde->bke", student_act, student_ada, preferred_element_type=F32)
    mods = jnp.stack([mod_t[:samples], mod_t[samples:], mod_s], axis=1)
    mods = jnp.pad(mods.reshape(4, 18, part), ((0, 0), (0, 6), (0, 128 - part)))
    mods = jnp.broadcast_to(mods[None], (4, 4, 24, 128)).reshape(16, 24, 128)
    mods = lax.all_to_all(mods, TENSOR, split_axis=0, concat_axis=0, tiled=True)
    mods = jnp.swapaxes(mods[:, :18, :part], 1, 2).reshape(width, 18)
    strengths = lax.dynamic_slice_in_dim(strength, quad * 2, 2, 0)

    nd = lambda s, d=BF16: jax.ShapeDtypeStruct(s, d)
    saved = []
    for i in range(2):
        col = i * 9
        saved.append(
            pl.pallas_call(
                functools.partial(student_kernel, i, col + 6, scale_norm),
                out_shape=(
                    nd((width, seq_len)), nd((width, seq_len)), nd((4 * QKV, seq_len)),
                    nd((4, seq_len, seq_len)), nd((4 * HD, seq_len)), nd((width, seq_len)),
                    nd((width, seq_len), F32),
                ),
                in_specs=[SM] + [VM] * 7,
                out_specs=(VM,) * 7,
                scratch_shapes=[pltpu.VMEM((width, seq_len), BF16)],
                compiler_params=params(28),
                cost_estimate=cost(5),
            )(pos, *tokens, mods, wq_s, wo_s)
        )
    cots = []
    for i in range(2):
        col = i * 9
        coef = jnp.stack([-(1.0 + strengths[i]), strengths[i]]) * scale_norm
        o0, o1, o3, o2 = pl.pallas_call(
            functools.partial(teacher_kernel, (col, col + 3)),
            grid=(2,),
            out_shape=(nd((block, seq_len)),) * 4,
            in_specs=[SM, SM] + [VM] * 5,
            out_specs=(VM,) * 4,
            scratch_shapes=[
                pltpu.VMEM((width, seq_len), F32),
                pltpu.VMEM((width, seq_len), BF16),
                pltpu.VMEM((4 * QKV, seq_len), BF16),
                pltpu.VMEM((4 * HD, seq_len), BF16),
            ],
            compiler_params=params(24, dimension_semantics=("arbitrary",)),
            cost_estimate=cost(9),
        )(pos, coef, saved[i][0], mods, wq_t, wo_t, saved[i][6])
        terms = [o0] + [lax.ppermute(o, "x", shifted(4, k)) for o, k in ((o1, 1), (o3, 3), (o2, 2))]
        cot = functools.reduce(jnp.add, [t.astype(F32) for t in terms]).astype(BF16)
        cots.append((cot,) + around(cot))

    back = []
    for i in range(2):
        normed, _, qkv, prob, mixed, proj, _ = saved[i]
        back.append(
            pl.pallas_call(
                functools.partial(backward_kernel, i * 9 + 6),
                out_shape=(nd((width, seq_len)), nd((4 * QKV, seq_len)), nd((8, width), F32)),
                in_specs=[SM] + [VM] * 12,
                out_specs=(VM,) * 3,
                scratch_shapes=[
                    pltpu.VMEM((width, seq_len), BF16),
                    pltpu.VMEM((4 * HD, seq_len), BF16),
                    pltpu.VMEM((width, 128), F32),
                ],
                compiler_params=params(28),
                cost_estimate=cost(6),
            )(pos, *cots[i], mods, wq_s, wo_s, normed, qkv, prob, mixed, proj)
        )

    gm = jnp.stack([back[0][2][:3], back[1][2][:3]], axis=1).reshape(6, width)
    gm = jnp.pad(gm, ((0, 2), (0, 0)))
    gm = jnp.concatenate([gm, lax.ppermute(gm, "core", xored(2, 1))], axis=0)
    gm = (gm,) + around(gm)
    acts = []
    for q in (quad, quad ^ 1):
        two = lax.dynamic_slice_in_dim(student_act, q * 2, 2, 0)
        acts += [two, two, two, jnp.zeros_like(two)]
    act_blocks = jnp.swapaxes(jnp.concatenate(acts, axis=0).reshape(16, 8, width // 8), 0, 1)
    act_blocks = jnp.pad(act_blocks, ((0, 0), (0, 0), (0, 256 - width // 8)))

    operands = []
    for i in range(2):
        operands += [saved[i][1], back[i][1], back[i][0], saved[i][4]]
    far1, far3, near0, near2 = pl.pallas_call(
        grads_kernel,
        out_shape=(nd((width, LANES)),) * 4,
        in_specs=[VM] * 8,
        out_specs=(VM,) * 4,
        compiler_params=params(24),
        cost_estimate=cost(4),
        name="grads",
    )(*operands)
    received = [lax.ppermute(v, "core", xored(2, 1)) for v in (far1, far3)]
    rows = width // 8
    pieces = pl.pallas_call(
        fold_kernel,
        out_shape=nd((16, rows // 6 * 7 + 16, 256)),
        in_specs=[SM] + [VM] * 9,
        out_specs=VM,
        compiler_params=params(16),
        cost_estimate=cost(2),
        name="fold",
    )(jnp.stack([x_at, zlo, core]).astype(jnp.int32), near0, near2, *received, act_blocks, *gm)
    summed = lax.all_to_all(pieces, ("zhi", "y", "zlo"), split_axis=0, concat_axis=0, tiled=True)
    grad_qkv, grad_out, grad_ada = pl.pallas_call(
        final_kernel,
        out_shape=(nd((rows, QKV), F32), nd((rows, HD), F32), nd((3, rows, HD), F32)),
        in_specs=[VM],
        out_specs=(VM, VM, VM),
        scratch_shapes=[pltpu.VMEM((256, 256), BF16)],
        compiler_params=params(12),
        cost_estimate=cost(1),
        name="final",
    )(summed)
    grad_out = grad_out.T

    return (grad_qkv, grad_out, grad_ada)


def solution(mesh):
    fine = Mesh(mesh.devices.reshape(SIZES), AXES)
    return jax.shard_map(
        local,
        mesh=fine,
        in_specs=(
            P(DP, None, TENSOR), P(DP), P(DP), P(DP), P(), P(), P(), P(),
            P(None, TENSOR), P(TENSOR, None), P(None, None, TENSOR),
            P(None, TENSOR), P(TENSOR, None), P(None, None, TENSOR),
        ),
        out_specs=(P(DP, TENSOR), P(TENSOR, DP), P(None, DP, TENSOR)),
        check_vma=False,
    )
```

time: 497 us -> 166 us (0.33)
  waiting for transfers between devices: 341 us -> 17 us
  matrix products: 57.8 us -> 4.87 us
  starting transfers between devices: 0.43 us -> 43.5 us
  Pallas kernels: 0 us -> 42.8 us
  between operations: 15.2 us -> 2.44 us
  local copies, waits for them, and re-layouts: 32.6 us -> 20.7 us
  blocking collectives: 36.5 us -> 28.1 us
  other arithmetic: 12.4 us -> 5.83 us
    unnamed x10 -> x0, waiting for transfers between devices: 274 us -> none
    all_gather x2 -> x0, waiting for transfers between devices: 67.6 us -> none  [the longest x1 42 us: local(): gathered = lax.all_gather(grad_proj, 'tensor', axis=2, tiled=True)]
    dot_general x20 -> x5, matrix products: 55.5 us -> 4.87 us  [the longest x2 2.26 us: lookup_rows(): return jnp.dot(one_hot, table_rows, preferred_element_type=F32)]
    pallas_call x0 -> x11, Pallas kernels: none -> 42.8 us  [the longest x2 15.4 us: local(): pl.pallas_call(functools.partial(teacher_kernel, (col, col + 3)), grid=(2...]
    ppermute x0 -> x36, starting transfers between devices: none -> 39 us  [the longest x12 19.5 us: around(): return tuple((lax.ppermute(v, 'x', shifted(4, k)) for k in (1, 3, 2)))]
    ppermute x0 -> x36, waiting for transfers between devices: none -> 17 us  [the longest x12 6.57 us: around(): return tuple((lax.ppermute(v, 'x', shifted(4, k)) for k in (1, 3, 2)))]
    all_to_all x3 -> x1, blocking collectives: 36.5 us -> 28.1 us  [local(): lax.all_to_all(pieces, ('zhi', 'y', 'zlo'), split_axis=0, concat_axis=0,...]
    unnamed x43 -> x65, local copies, waits for them, and re-layouts: 19.9 us -> 11.6 us
  transfers between devices with their start and end apart: 6 -> 37, of which waited for: 6 -> 12; matrix products, arithmetic and copies ran while one was open for 10% -> 10% of each run, Pallas kernels for 0% -> 12%
where the time goes in v1:
time: 166 us; the launch traced here: 165 us
  starting transfers between devices  43.5 us (26%)
  Pallas kernels  42.8 us (26%)
  blocking collectives  28.1 us (17%)
  local copies, waits for them, and re-layouts  20.7 us (12%)
  waiting for transfers between devices  17 us (10%)
  other arithmetic  5.83 us (4%)
  matrix products  4.87 us (3%)
  between operations  2.44 us (1%)
    all_to_all x1, blocking collectives, local(): lax.all_to_all(pieces, ('zhi', 'y', 'zlo'), split_axis=0, concat_axis=0,...  28.1 us
    ppermute x12, starting transfers between devices, around(): return tuple((lax.ppermute(v, 'x', shifted(4, k)) for k in (1, 3, 2)))  19.5 us
    pallas_call x2, Pallas kernels, local(): pl.pallas_call(functools.partial(teacher_kernel, (col, col + 3)), grid=(2...  15.4 us
    unnamed x65, local copies, waits for them, and re-layouts  11.6 us
    pallas_call x2, Pallas kernels, local(): pl.pallas_call(functools.partial(student_kernel, i, col + 6, scale_norm),...  9.56 us
    ppermute x6, starting transfers between devices, local(): lax.ppermute(o, 'x', shifted(4, k))  8.93 us
    ppermute x12, waiting for transfers between devices, around(): return tuple((lax.ppermute(v, 'x', shifted(4, k)) for k in (1, 3, 2)))  6.57 us
    pallas_call x2, Pallas kernels, local(): pl.pallas_call(functools.partial(backward_kernel, i * 9 + 6), out_shape=(...  6.31 us
  transfers between devices with their start and end apart: 37, of which 12 were waited for; matrix products, arithmetic and copies ran while one was open for 10% of the time, Pallas kernels for 12%

profile of v1, /device:TPU:0, one launch (start us, length us, event | category | flops | bytes accessed | tf_op | source)
XLA Modules:
  0.0 165.4 jit_solution(5897351266585603807)
XLA Ops:
  10.5 1.9 %collective-permute-start.14 = (bf16[216,1152]{1,0:T(8,128)(2,1)S(1)}, bf16[216,1152]{1,0:T(8,128)(2,1)}, u32[]{:S(2)}, u32[]{:S(2)}) collective-permute-start(bf16[216,1152]{1,0:T(8,128)(2,1)S(1)} %bitcast.49), channel_id=1, source_target_pairs={{0,2},{2,64},{64,66},{66,0},{1,3},{3,65},{65,67},{67,1},{4,6},{6,6... | collective-permute-start | bytes 1493000 | tf_op jit(solution)/shard_map/ppermute | solution.py:274
  13.5 2.2 %collective-permute-start.8 = (bf16[216,1152]{1,0:T(8,128)(2,1)}, bf16[216,1152]{1,0:T(8,128)(2,1)}, u32[]{:S(2)}, u32[]{:S(2)}) collective-permute-start(bf16[216,1152]{1,0:T(8,128)(2,1)} %bitcast.15.refs_0_), channel_id=1, source_target_pairs={{0,66},{2,0},{64,2},{66,64},{1,67},{3,1},{65,3},{67,65},{4,70},{6,... | collective-permute-start | bytes 1493000 | tf_op jit(solution)/shard_map/ppermute | solution.py:274
  15.7 2.1 %collective-permute-start.9 = (bf16[72,1152]{1,0:T(8,128)(2,1)S(1)}, bf16[72,1152]{1,0:T(8,128)(2,1)S(1)}, u32[]{:S(2)}, u32[]{:S(2)}) collective-permute-start(bf16[72,1152]{1,0:T(8,128)(2,1)S(1)} %copy-done.11), channel_id=1, source_target_pairs={{0,66},{2,0},{64,2},{66,64},{1,67},{3,1},{65,3},{67,65},{4,70},{6,... | collective-permute-start | bytes 497672 | tf_op jit(solution)/shard_map/ppermute | solution.py:274
  22.7 4.6 %all-to-all-start = ((f32[16,24,128]{2,1,0:T(8,128)}), f32[16,24,128]{2,1,0:T(8,128)}, u32[]{:S(2)}, u32[]{:S(2)}) async-start(f32[16,24,128]{2,1,0:T(8,128)} %bitcast.53), calls=%async_computation | async-start | bytes 393216 | tf_op jit(solution)/shard_map/all_to_all | solution.py:334
  27.3 3.2 %collective-permute-done.9.refs_5_ = bf16[72,1152]{1,0:T(8,128)(2,1)S(1)} collective-permute-done((bf16[72,1152]{1,0:T(8,128)(2,1)S(1)}, bf16[72,1152]{1,0:T(8,128)(2,1)S(1)}, u32[]{:S(2)}, u32[]{:S(2)}) %collective-permute-start.9) | collective-permute-done | bytes 165920 | tf_op jit(solution)/shard_map/ppermute | solution.py:274
  38.0 3.3 %collective-permute-start.5 = (bf16[2,288,256]{2,1,0:T(8,128)(2,1)S(1)}, bf16[2,288,256]{2,1,0:T(8,128)(2,1)S(1)}, u32[]{:S(2)}, u32[]{:S(2)}) collective-permute-start(bf16[2,288,256]{2,1,0:T(8,128)(2,1)S(1)} %pad_maximum_fusion.p0), channel_id=1, source_target_pairs={{0,8},{4,12},{8,0},{12,4},{1,9},{5,13},{9,1},{13,5},{2,10},{6,14},... | collective-permute-start | bytes 884744 | tf_op jit(solution)/shard_map/ppermute | solution.py:268
  54.9 2.2 %shard_map.159 = (bf16[864,1152]{1,0:T(8,128)(2,1)S(1)}, bf16[288,1152]{1,0:T(8,128)(2,1)S(1)}) custom-call(bf16[216,1152]{1,0:T(8,128)(2,1)S(1)} %bitcast.51, bf16[72,1152]{1,0:T(8,128)(2,1)S(1)} %copy-done.10, bf16[216,1152]{1,0:T(8,128)(2,1)S(1)} %copy-done.6, bf16[72,1152]{1,0:T(8,128)(2,1)S(1)} %copy-done.20, ...), custom_call_target="tpu_custom_call" | custom-call | flops 200000000 | bytes 1000000 | tf_op jit(solution)/shard_map/pallas_call | solution.py:277
  57.2 1.9 %shard_map.157 = (bf16[864,1152]{1,0:T(8,128)(2,1)S(1)}, bf16[288,1152]{1,0:T(8,128)(2,1)S(1)}) custom-call(bf16[216,1152]{1,0:T(8,128)(2,1)} %bitcast.15.refs_0_, bf16[72,1152]{1,0:T(8,128)(2,1)S(1)} %copy-done.12, bf16[216,1152]{1,0:T(8,128)(2,1)} %collective-permute-done.6.refs_2_, bf16[72,1152]{1,0:T(8,128)(2,1)S(1)} %copy-done.16, ...), custom_call_target="tpu_custom_call" | custom-call | flops 200000000 | bytes 1000000 | tf_op jit(solution)/shard_map/pallas_call | solution.py:277
  59.1 4.8 %shard_map.162 = (bf16[1152,256]{1,0:T(8,128)(2,1)S(1)}, bf16[1152,256]{1,0:T(8,128)(2,1)S(1)}, bf16[864,256]{1,0:T(8,128)(2,1)S(1)}, bf16[4,256,256]{2,1,0:T(8,...) custom-call(s32[1]{0:T(128)} %bitcast.pos_ref, ...), custom_call_target="tpu_custom_call" | custom-call | flops 500000000 | bytes 1000000 | tf_op jit(solution)/shard_map/pallas_call | solution.py:343
  63.9 7.7 %shard_map.163 = (bf16[288,256]{1,0:T(8,128)(2,1)S(1)}, bf16[288,256]{1,0:T(8,128)(2,1)S(1)}, bf16[288,256]{1,0:T(8,128)(2,1)S(1)}, bf16[288,256]{1,0:T(8,128)(2,1)S(1)}) custom-call(s32[1]{0:T(128)} %bitcast.pos_ref, f32[2]{0:T(128)S(1)} %get-tuple-element.120.coef_ref, bf16[1152,256]{1,0:T(8,128)(2,1)S(1)} %get-tuple-element.68.normed_ref, ...), custom_call_target="tpu_custom_call" | custom-call | flops 900000000 | bytes 1000000 | tf_op jit(solution)/shard_map/pallas_call | solution.py:361
  72.7 2.2 %collective-permute-start.25 = (bf16[288,256]{1,0:T(8,128)(2,1)S(1)}, bf16[288,256]{1,0:T(8,128)(2,1)S(1)}, u32[]{:S(2)}, u32[]{:S(2)}) collective-permute-start(bf16[288,256]{1,0:T(8,128)(2,1)S(1)} %get-tuple-element.72), channel_id=1, source_target_pairs={{0,12},{4,0},{8,4},{12,8},{1,13},{5,1},{9,5},{13,9},{2,14},{6,2},{... | collective-permute-start | bytes 442376 | tf_op jit(solution)/shard_map/ppermute | solution.py:376
  75.2 4.8 %shard_map.158 = (bf16[1152,256]{1,0:T(8,128)(2,1)S(1)}, bf16[1152,256]{1,0:T(8,128)(2,1)S(1)}, bf16[864,256]{1,0:T(8,128)(2,1)S(1)}, bf16[4,256,256]{2,1,0:T(8,...) custom-call(s32[1]{0:T(128)} %bitcast.pos_ref, ...), custom_call_target="tpu_custom_call" | custom-call | flops 500000000 | bytes 1000000 | tf_op jit(solution)/shard_map/pallas_call | solution.py:343
  80.0 7.7 %shard_map.160 = (bf16[288,256]{1,0:T(8,128)(2,1)S(1)}, bf16[288,256]{1,0:T(8,128)(2,1)S(1)}, bf16[288,256]{1,0:T(8,128)(2,1)S(1)}, bf16[288,256]{1,0:T(8,128)(2,1)S(1)}) custom-call(s32[1]{0:T(128)} %bitcast.pos_ref, f32[2]{0:T(128)S(1)} %get-tuple-element.119.coef_ref, bf16[1152,256]{1,0:T(8,128)(2,1)S(1)} %get-tuple-element.51.normed_ref, ...), custom_call_target="tpu_custom_call" | custom-call | flops 900000000 | bytes 1000000 | tf_op jit(solution)/shard_map/pallas_call | solution.py:361
  91.0 2.0 %collective-permute-start.20 = (bf16[288,256]{1,0:T(8,128)(2,1)S(1)}, bf16[288,256]{1,0:T(8,128)(2,1)S(1)}, u32[]{:S(2)}, u32[]{:S(2)}) collective-permute-start(bf16[288,256]{1,0:T(8,128)(2,1)S(1)} %get-tuple-element.60), channel_id=1, source_target_pairs={{0,8},{4,12},{8,0},{12,4},{1,9},{5,13},{9,1},{13,5},{2,10},{6,14},... | collective-permute-start | bytes 442376 | tf_op jit(solution)/shard_map/ppermute | solution.py:376
  96.8 2.0 %collective-permute-done.19 = bf16[288,256]{1,0:T(8,128)(2,1)S(1)} collective-permute-done((bf16[288,256]{1,0:T(8,128)(2,1)S(1)}, bf16[288,256]{1,0:T(8,128)(2,1)S(1)}, u32[]{:S(2)}, u32[]{:S(2)}) %collective-permute-start.19) | collective-permute-done | bytes 147488 | tf_op jit(solution)/shard_map/ppermute | solution.py:376
  99.4 2.0 %collective-permute-start.23 = (bf16[288,256]{1,0:T(8,128)(2,1)S(1)}, bf16[288,256]{1,0:T(8,128)(2,1)S(1)}, u32[]{:S(2)}, u32[]{:S(2)}) collective-permute-start(bf16[288,256]{1,0:T(8,128)(2,1)S(1)} %add_convert_fusion.1.p0), channel_id=1, source_target_pairs={{0,8},{4,12},{8,0},{12,4},{1,9},{5,13},{9,1},{13,5},{2,10},{6,14},... | collective-permute-start | bytes 442376 | tf_op jit(solution)/shard_map/ppermute | solution.py:268
  101.4 4.1 %collective-permute-start.22 = (bf16[288,256]{1,0:T(8,128)(2,1)S(1)}, bf16[288,256]{1,0:T(8,128)(2,1)S(1)}, u32[]{:S(2)}, u32[]{:S(2)}) collective-permute-start(bf16[288,256]{1,0:T(8,128)(2,1)S(1)} %add_convert_fusion.1.p0), channel_id=1, source_target_pairs={{0,12},{4,0},{8,4},{12,8},{1,13},{5,1},{9,5},{13,9},{2,14},{6,2},{... | collective-permute-start | bytes 442376 | tf_op jit(solution)/shard_map/ppermute | solution.py:268
  106.8 3.2 %shard_map.164 = (bf16[1152,256]{1,0:T(8,128)(2,1)S(1)}, bf16[864,256]{1,0:T(8,128)(2,1)S(1)}, f32[8,1152]{1,0:T(8,128)S(1)}) custom-call(s32[1]{0:T(128)} %bitcast.pos_ref, bf16[288,256]{1,0:T(8,128)(2,1)S(1)} %add_convert_fusion.p0, bf16[288,256]{1,0:T(8,128)(2,1)S(1)} %collective-permute-done.27.p1, bf16[288,256]{1,0:T(8,128)(2,1)S(1)} %collective-permute-done.28.p2, ...), custom_call_target="tpu_custom_call" | custom-call | flops 600000000 | bytes 1000000 | tf_op jit(solution)/shard_map/pallas_call | solution.py:384
  111.9 3.2 %shard_map.161 = (bf16[1152,256]{1,0:T(8,128)(2,1)S(1)}, bf16[864,256]{1,0:T(8,128)(2,1)S(1)}, f32[8,1152]{1,0:T(8,128)S(1)}) custom-call(s32[1]{0:T(128)} %bitcast.pos_ref, bf16[288,256]{1,0:T(8,128)(2,1)S(1)} %add_convert_fusion.1.p0, bf16[288,256]{1,0:T(8,128)(2,1)S(1)} %collective-permute-done.21.p1, bf16[288,256]{1,0:T(8,128)(2,1)S(1)} %collective-permute-done.22.p2, ...), custom_call_target="tpu_custom_call" | custom-call | flops 600000000 | bytes 1000000 | tf_op jit(solution)/shard_map/pallas_call | solution.py:384
  115.0 3.1 %grads.1 = (bf16[1152,384]{1,0:T(8,128)(2,1)}, bf16[1152,384]{1,0:T(8,128)(2,1)}, bf16[1152,384]{1,0:T(8,128)(2,1)S(1)}, bf16[1152,384]{1,0:T(8,128)(2,1)S(1)}) custom-call(bf16[1152,256]{1,0:T(8,128)(2,1)S(1)} %get-tuple-element.50.m0, bf16[864,256]{1,0:T(8,128)(2,1)S(1)} %get-tuple-element.65.g0, bf16[1152,256]{1,0:T(8,128)(2,1)S(1)} %get-tuple-element.66.p0, ...), custom_call_target="tpu_custom_call" | custom-call | flops 400000000 | bytes 1000000 | tf_op jit(solution)/shard_map/grads/pallas_call | solution.py:413
  120.1 3.0 %collective-permute-done.32 = f32[8,1152]{1,0:T(8,128)S(1)} collective-permute-done((f32[8,1152]{1,0:T(8,128)S(1)}, f32[8,1152]{1,0:T(8,128)S(1)}, u32[]{:S(2)}, u32[]{:S(2)}) %collective-permute-start.32) | collective-permute-done | bytes 36896 | tf_op jit(solution)/shard_map/ppermute | solution.py:401
  126.9 2.3 %collective-permute-done.35.a3 = f32[16,1152]{1,0:T(8,128)S(1)} collective-permute-done((f32[16,1152]{1,0:T(8,128)S(1)}, f32[16,1152]{1,0:T(8,128)S(1)}, u32[]{:S(2)}, u32[]{:S(2)}) %collective-permute-start.35) | collective-permute-done | bytes 73760 | tf_op jit(solution)/shard_map/ppermute | solution.py:268
  132.2 3.3 %fold.1 = bf16[16,184,256]{2,1,0:T(8,128)(2,1)S(1)} custom-call(s32[3]{0:T(128)S(1)} %pad_add_fusion.at_ref, bf16[1152,384]{1,0:T(8,128)(2,1)S(1)} %get-tuple-element.80.s0, bf16[1152,384]{1,0:T(8,128)(2,1)S(1)} %copy-done.2, bf16[1152,384]{1,0:T(8,128)(2,1)} %collective-permute-done.30.r1, bf16[1152,384]{1,0:T(8,128)(2,1)} %collective-permute-done.31.r3, ...), custom_call_target="tpu_custom_call" | custom-call | flops 200000000 | bytes 1000000 | tf_op jit(solution)/shard_map/fold/pallas_call | solution.py:424
  135.5 28.1 %all_to_all.10.in_ref = bf16[16,184,256]{2,1,0:T(8,128)(2,1)S(1)} all-to-all(bf16[16,184,256]{2,1,0:T(8,128)(2,1)S(1)} %fold.1), channel_id=1, replica_groups=mesh['zhi'=2,'y'=4,'x'=4,'zlo'=2,'core'=2] {'zhi','y','zlo'}, dimensions={0} | all-to-all | bytes 3014656 | tf_op jit(solution)/shard_map/all_to_all | solution.py:433
  (165 shorter events, 58.3 us)
Async XLA Ops:
  10.5 20.6 %collective-permute-start.14 = (bf16[216,1152]{1,0:T(8,128)(2,1)S(1)}, bf16[216,1152]{1,0:T(8,128)(2,1)}, u32[]{:S(2)}, u32[]{:S(2)}) collective-permute-start(bf16[216,1152]{1,0:T(8,128)(2,1)S(1)} %bitcast.49), channel_id=1, source_target_pairs={{0,2},{2,64},{64,66},{66,0},{1,3},{3,65},{65,67},{67,1},{4,6},{6,6... | collective-permute-start | bytes 1493000 | tf_op jit(solution)/shard_map/ppermute | solution.py:274
  13.5 22.0 %collective-permute-start.8 = (bf16[216,1152]{1,0:T(8,128)(2,1)}, bf16[216,1152]{1,0:T(8,128)(2,1)}, u32[]{:S(2)}, u32[]{:S(2)}) collective-permute-start(bf16[216,1152]{1,0:T(8,128)(2,1)} %bitcast.15.refs_0_), channel_id=1, source_target_pairs={{0,66},{2,0},{64,2},{66,64},{1,67},{3,1},{65,3},{67,65},{4,70},{6,... | collective-permute-start | bytes 1493000 | tf_op jit(solution)/shard_map/ppermute | solution.py:274
  15.7 14.8 %collective-permute-start.9 = (bf16[72,1152]{1,0:T(8,128)(2,1)S(1)}, bf16[72,1152]{1,0:T(8,128)(2,1)S(1)}, u32[]{:S(2)}, u32[]{:S(2)}) collective-permute-start(bf16[72,1152]{1,0:T(8,128)(2,1)S(1)} %copy-done.11), channel_id=1, source_target_pairs={{0,66},{2,0},{64,2},{66,64},{1,67},{3,1},{65,3},{67,65},{4,70},{6,... | collective-permute-start | bytes 497672 | tf_op jit(solution)/shard_map/ppermute | solution.py:274
  17.8 12.7 %collective-permute-start.7 = (bf16[72,1152]{1,0:T(8,128)(2,1)S(1)}, bf16[72,1152]{1,0:T(8,128)(2,1)S(1)}, u32[]{:S(2)}, u32[]{:S(2)}) collective-permute-start(bf16[72,1152]{1,0:T(8,128)(2,1)S(1)} %copy-done.11), channel_id=1, source_target_pairs={{0,1},{1,0},{2,3},{3,2},{4,5},{5,4},{6,7},{7,6},{8,9},{9,8},{10,11... | collective-permute-start | bytes 497672 | tf_op jit(solution)/shard_map/ppermute | solution.py:273
  17.8 13.2 %collective-permute-start.15 = (bf16[72,1152]{1,0:T(8,128)(2,1)S(1)}, bf16[72,1152]{1,0:T(8,128)(2,1)}, u32[]{:S(2)}, u32[]{:S(2)}) collective-permute-start(bf16[72,1152]{1,0:T(8,128)(2,1)S(1)} %copy-done.9), channel_id=1, source_target_pairs={{0,2},{2,64},{64,66},{66,0},{1,3},{3,65},{65,67},{67,1},{4,6},{6,6... | collective-permute-start | bytes 497672 | tf_op jit(solution)/shard_map/ppermute | solution.py:274
  22.7 23.5 %all-to-all-start = ((f32[16,24,128]{2,1,0:T(8,128)}), f32[16,24,128]{2,1,0:T(8,128)}, u32[]{:S(2)}, u32[]{:S(2)}) async-start(f32[16,24,128]{2,1,0:T(8,128)} %bitcast.53), calls=%async_computation | async-start | bytes 393216 | tf_op jit(solution)/shard_map/all_to_all | solution.py:334
  30.5 10.8 %collective-permute-start.12 = (bf16[216,1152]{1,0:T(8,128)(2,1)S(1)}, bf16[216,1152]{1,0:T(8,128)(2,1)S(1)}, u32[]{:S(2)}, u32[]{:S(2)}) collective-permute-start(bf16[216,1152]{1,0:T(8,128)(2,1)S(1)} %bitcast.50), channel_id=1, source_target_pairs={{0,1},{1,0},{2,3},{3,2},{4,5},{5,4},{6,7},{7,6},{8,9},{9,8},{10,11... | collective-permute-start | bytes 1493000 | tf_op jit(solution)/shard_map/ppermute | solution.py:273
  31.1 11.9 %collective-permute-start.16 = (bf16[216,1152]{1,0:T(8,128)(2,1)}, bf16[216,1152]{1,0:T(8,128)(2,1)S(1)}, u32[]{:S(2)}, u32[]{:S(2)}) collective-permute-start(bf16[216,1152]{1,0:T(8,128)(2,1)} %collective-permute-done.14.refs_4_), channel_id=1, source_target_pairs={{0,1},{1,0},{2,3},{3,2},{4,5},{5,4},{6,7},{7,6},{8,9},{9,8},{10,11... | collective-permute-start | bytes 1493000 | tf_op jit(solution)/shard_map/ppermute | solution.py:275
  35.0 22.1 %collective-permute-start.6 = (bf16[216,1152]{1,0:T(8,128)(2,1)}, bf16[216,1152]{1,0:T(8,128)(2,1)}, u32[]{:S(2)}, u32[]{:S(2)}) collective-permute-start(bf16[216,1152]{1,0:T(8,128)(2,1)} %bitcast.15.refs_0_), channel_id=1, source_target_pairs={{0,1},{1,0},{2,3},{3,2},{4,5},{5,4},{6,7},{7,6},{8,9},{9,8},{10,11... | collective-permute-start | bytes 1493000 | tf_op jit(solution)/shard_map/ppermute | solution.py:273
  35.5 21.6 %collective-permute-start.10 = (bf16[216,1152]{1,0:T(8,128)(2,1)}, bf16[216,1152]{1,0:T(8,128)(2,1)}, u32[]{:S(2)}, u32[]{:S(2)}) collective-permute-start(bf16[216,1152]{1,0:T(8,128)(2,1)} %collective-permute-done.8.refs_4_), channel_id=1, source_target_pairs={{0,1},{1,0},{2,3},{3,2},{4,5},{5,4},{6,7},{7,6},{8,9},{9,8},{10,11... | collective-permute-start | bytes 1493000 | tf_op jit(solution)/shard_map/ppermute | solution.py:275
  38.0 21.0 %collective-permute-start.5 = (bf16[2,288,256]{2,1,0:T(8,128)(2,1)S(1)}, bf16[2,288,256]{2,1,0:T(8,128)(2,1)S(1)}, u32[]{:S(2)}, u32[]{:S(2)}) collective-permute-start(bf16[2,288,256]{2,1,0:T(8,128)(2,1)S(1)} %pad_maximum_fusion.p0), channel_id=1, source_target_pairs={{0,8},{4,12},{8,0},{12,4},{1,9},{5,13},{9,1},{13,5},{2,10},{6,14},... | collective-permute-start | bytes 884744 | tf_op jit(solution)/shard_map/ppermute | solution.py:268
  42.1 16.9 %collective-permute-start.4 = (bf16[2,288,256]{2,1,0:T(8,128)(2,1)S(1)}, bf16[2,288,256]{2,1,0:T(8,128)(2,1)}, u32[]{:S(2)}, u32[]{:S(2)}) collective-permute-start(bf16[2,288,256]{2,1,0:T(8,128)(2,1)S(1)} %pad_maximum_fusion.p0), channel_id=1, source_target_pairs={{0,12},{4,0},{8,4},{12,8},{1,13},{5,1},{9,5},{13,9},{2,14},{6,2},{... | collective-permute-start | bytes 884744 | tf_op jit(solution)/shard_map/ppermute | solution.py:268
  43.8 15.3 %collective-permute-start.3 = (bf16[2,288,256]{2,1,0:T(8,128)(2,1)S(1)}, bf16[2,288,256]{2,1,0:T(8,128)(2,1)}, u32[]{:S(2)}, u32[]{:S(2)}) collective-permute-start(bf16[2,288,256]{2,1,0:T(8,128)(2,1)S(1)} %pad_maximum_fusion.p0), channel_id=1, source_target_pairs={{0,4},{4,8},{8,12},{12,0},{1,5},{5,9},{9,13},{13,1},{2,6},{6,10},{... | collective-permute-start | bytes 884744 | tf_op jit(solution)/shard_map/ppermute | solution.py:268
  71.6 19.5 %collective-permute-start.24 = (bf16[288,256]{1,0:T(8,128)(2,1)S(1)}, bf16[288,256]{1,0:T(8,128)(2,1)S(1)}, u32[]{:S(2)}, u32[]{:S(2)}) collective-permute-start(bf16[288,256]{1,0:T(8,128)(2,1)S(1)} %get-tuple-element.71), channel_id=1, source_target_pairs={{0,4},{4,8},{8,12},{12,0},{1,5},{5,9},{9,13},{13,1},{2,6},{6,10},{... | collective-permute-start | bytes 442376 | tf_op jit(solution)/shard_map/ppermute | solution.py:376
  72.7 20.3 %collective-permute-start.25 = (bf16[288,256]{1,0:T(8,128)(2,1)S(1)}, bf16[288,256]{1,0:T(8,128)(2,1)S(1)}, u32[]{:S(2)}, u32[]{:S(2)}) collective-permute-start(bf16[288,256]{1,0:T(8,128)(2,1)S(1)} %get-tuple-element.72), channel_id=1, source_target_pairs={{0,12},{4,0},{8,4},{12,8},{1,13},{5,1},{9,5},{13,9},{2,14},{6,2},{... | collective-permute-start | bytes 442376 | tf_op jit(solution)/shard_map/ppermute | solution.py:376
  74.9 18.1 %collective-permute-start.26 = (bf16[288,256]{1,0:T(8,128)(2,1)S(1)}, bf16[288,256]{1,0:T(8,128)(2,1)S(1)}, u32[]{:S(2)}, u32[]{:S(2)}) collective-permute-start(bf16[288,256]{1,0:T(8,128)(2,1)S(1)} %get-tuple-element.73), channel_id=1, source_target_pairs={{0,8},{4,12},{8,0},{12,4},{1,9},{5,13},{9,1},{13,5},{2,10},{6,14},... | collective-permute-start | bytes 442376 | tf_op jit(solution)/shard_map/ppermute | solution.py:376
  89.2 9.5 %collective-permute-start.19 = (bf16[288,256]{1,0:T(8,128)(2,1)S(1)}, bf16[288,256]{1,0:T(8,128)(2,1)S(1)}, u32[]{:S(2)}, u32[]{:S(2)}) collective-permute-start(bf16[288,256]{1,0:T(8,128)(2,1)S(1)} %get-tuple-element.59), channel_id=1, source_target_pairs={{0,12},{4,0},{8,4},{12,8},{1,13},{5,1},{9,5},{13,9},{2,14},{6,2},{... | collective-permute-start | bytes 442376 | tf_op jit(solution)/shard_map/ppermute | solution.py:376
  93.1 12.4 %collective-permute-start.29 = (bf16[288,256]{1,0:T(8,128)(2,1)S(1)}, bf16[288,256]{1,0:T(8,128)(2,1)S(1)}, u32[]{:S(2)}, u32[]{:S(2)}) collective-permute-start(bf16[288,256]{1,0:T(8,128)(2,1)S(1)} %add_convert_fusion.p0), channel_id=1, source_target_pairs={{0,8},{4,12},{8,0},{12,4},{1,9},{5,13},{9,1},{13,5},{2,10},{6,14},... | collective-permute-start | bytes 442376 | tf_op jit(solution)/shard_map/ppermute | solution.py:268
  94.7 11.6 %collective-permute-start.28 = (bf16[288,256]{1,0:T(8,128)(2,1)S(1)}, bf16[288,256]{1,0:T(8,128)(2,1)S(1)}, u32[]{:S(2)}, u32[]{:S(2)}) collective-permute-start(bf16[288,256]{1,0:T(8,128)(2,1)S(1)} %add_convert_fusion.p0), channel_id=1, source_target_pairs={{0,12},{4,0},{8,4},{12,8},{1,13},{5,1},{9,5},{13,9},{2,14},{6,2},{... | collective-permute-start | bytes 442376 | tf_op jit(solution)/shard_map/ppermute | solution.py:268
  95.7 11.1 %collective-permute-start.27 = (bf16[288,256]{1,0:T(8,128)(2,1)S(1)}, bf16[288,256]{1,0:T(8,128)(2,1)S(1)}, u32[]{:S(2)}, u32[]{:S(2)}) collective-permute-start(bf16[288,256]{1,0:T(8,128)(2,1)S(1)} %add_convert_fusion.p0), channel_id=1, source_target_pairs={{0,4},{4,8},{8,12},{12,0},{1,5},{5,9},{9,13},{13,1},{2,6},{6,10},{... | collective-permute-start | bytes 442376 | tf_op jit(solution)/shard_map/ppermute | solution.py:268
  99.4 10.5 %collective-permute-start.23 = (bf16[288,256]{1,0:T(8,128)(2,1)S(1)}, bf16[288,256]{1,0:T(8,128)(2,1)S(1)}, u32[]{:S(2)}, u32[]{:S(2)}) collective-permute-start(bf16[288,256]{1,0:T(8,128)(2,1)S(1)} %add_convert_fusion.1.p0), channel_id=1, source_target_pairs={{0,8},{4,12},{8,0},{12,4},{1,9},{5,13},{9,1},{13,5},{2,10},{6,14},... | collective-permute-start | bytes 442376 | tf_op jit(solution)/shard_map/ppermute | solution.py:268
  101.4 9.6 %collective-permute-start.22 = (bf16[288,256]{1,0:T(8,128)(2,1)S(1)}, bf16[288,256]{1,0:T(8,128)(2,1)S(1)}, u32[]{:S(2)}, u32[]{:S(2)}) collective-permute-start(bf16[288,256]{1,0:T(8,128)(2,1)S(1)} %add_convert_fusion.1.p0), channel_id=1, source_target_pairs={{0,12},{4,0},{8,4},{12,8},{1,13},{5,1},{9,5},{13,9},{2,14},{6,2},{... | collective-permute-start | bytes 442376 | tf_op jit(solution)/shard_map/ppermute | solution.py:268
  119.1 11.9 %collective-permute-start.30 = (bf16[1152,384]{1,0:T(8,128)(2,1)}, bf16[1152,384]{1,0:T(8,128)(2,1)}, u32[]{:S(2)}, u32[]{:S(2)}) collective-permute-start(bf16[1152,384]{1,0:T(8,128)(2,1)} %get-tuple-element.82), channel_id=1, source_target_pairs={{0,1},{1,0},{2,3},{3,2},{4,5},{5,4},{6,7},{7,6},{8,9},{9,8},{10,11... | collective-permute-start | bytes 2654216 | tf_op jit(solution)/shard_map/ppermute | solution.py:422
  119.1 11.9 %collective-permute-start.31 = (bf16[1152,384]{1,0:T(8,128)(2,1)}, bf16[1152,384]{1,0:T(8,128)(2,1)}, u32[]{:S(2)}, u32[]{:S(2)}) collective-permute-start(bf16[1152,384]{1,0:T(8,128)(2,1)} %get-tuple-element.83), channel_id=1, source_target_pairs={{0,1},{1,0},{2,3},{3,2},{4,5},{5,4},{6,7},{7,6},{8,9},{9,8},{10,11... | collective-permute-start | bytes 2654216 | tf_op jit(solution)/shard_map/ppermute | solution.py:422
  (45 other events, 182.0 us)
